TPU v7x, 32 devices: a whole 2x2x4 slice. The times are simulated.
32 devices in a mesh: lev: 4 (over y, x), col: 8 (over z, core).
Axes of the slice: x: 2, y: 2, z: 4, core: 2. Of those that a mesh axis runs over, the one named last changes fastest.
Arguments:
- control_field: float32 [96, 16, 192, 128], P('lev', None, 'col'), may hold values from -24 to 24
- decay_rate: float32 [96, 192, 128], P('lev', 'col'), may hold values from 0.5 to 0.999
- diffusivity: float32 [192, 128], P('col'), may hold values from 0.08 to 0.24
Outputs:
- localized: float32 [96, 16, 192, 128], P('lev', None, 'col')
All inputs are finite; a program needn't handle non-finite values.
Results may differ from a plain program's by a relative error of at most 0.00002.
Values sent between devices are 32-bit elements; how exact they have to be, the bound alone decides.
A program may use at most 64 MiB of HBM per device.

v0:
```python
import jax
import jax.numpy as jnp
from jax import lax
from jax.sharding import PartitionSpec as P

SMOOTH = 4


def entering_2(x, axis, combine, identity, reverse):
    peers, here = (lax.axis_size(axis), lax.axis_index(axis))
    everything = jax.tree.map(lambda part: lax.all_gather(part, axis), x)
    start = jax.tree.map(
        lambda part, zero: jnp.broadcast_to(jnp.asarray(zero, part.dtype), part.shape), x, identity
    )

    def hop(k, before):
        at = peers - 1 - k if reverse else k
        reached = at > here if reverse else at < here
        new = combine(before, jax.tree.map(lambda part: part[at], everything))
        return jax.tree.map(lambda a, b: jnp.where(reached, a, b), new, before)

    return lax.fori_loop(0, peers, hop, start)


def with_halo(block, sides, width):
    for axis, dim in sides:
        count = lax.axis_size(axis)
        forward = [(i, i + 1) for i in range(count - 1)]
        backward = [(target, source) for source, target in forward]
        low = lax.ppermute(
            lax.slice_in_dim(block, block.shape[dim] - width, None, axis=dim), axis, forward
        )
        high = lax.ppermute(lax.slice_in_dim(block, 0, width, axis=dim), axis, backward)
        block = jnp.concatenate([low, block, high], axis=dim)
    return block


def sweep_levels(decay_rates, field, backward):
    blocks = field.shape[0] // 8
    rate_blocks = decay_rates.reshape((blocks, 8) + decay_rates.shape[1:])
    field_blocks = field.reshape((blocks, 8) + field.shape[1:])

    def run_block(state, inputs):
        rate_block, values_block = inputs
        results = [None] * 8
        order = range(7, -1, -1) if backward else range(8)
        for position in order:
            weight = rate_block[position]
            state = weight * state + (1.0 - weight) * values_block[position]
            results[position] = state
        return (state, jnp.stack(results))

    start = jnp.zeros(field.shape[1:], jnp.float32)
    unused, swept = lax.scan(run_block, start, (rate_blocks, field_blocks), reverse=backward)
    return swept.reshape(field.shape)


def combine_maps(earlier, later):
    return (later[0] * earlier[0], later[0][None] * earlier[1] + later[1])


def forward_pass(decay_rates, field):
    within = sweep_levels(decay_rates, field, False)
    through = jnp.prod(decay_rates, axis=0)
    identity = (jnp.ones_like(through), jnp.zeros_like(within[-1]))
    entering = entering_2((through, within[-1]), "lev", combine_maps, identity, False)
    growth = jnp.cumprod(decay_rates, axis=0)
    return within + growth[:, None] * entering[1][None]


def backward_pass(decay_rates, field):
    within = sweep_levels(decay_rates, field, True)
    through = jnp.prod(decay_rates, axis=0)
    identity = (jnp.ones_like(through), jnp.zeros_like(within[0]))
    entering = entering_2((through, within[0]), "lev", combine_maps, identity, True)
    growth = jnp.flip(jnp.cumprod(jnp.flip(decay_rates, 0), axis=0), 0)
    return within + growth[:, None] * entering[1][None]


def lat_sum(field):
    padded = jnp.pad(field, ((0, 0), (0, 0), (0, 0), (1, 1)))
    return padded[..., 2:] + padded[..., :-2]


def per_device(control_field, decay_rate, diffusivity):
    filtered = control_field
    for repeat in range(2):
        filtered = forward_pass(decay_rate, filtered)
        filtered = backward_pass(decay_rate, filtered)
    current = with_halo(filtered, (("col", 2),), SMOOTH)
    kappa_wide = with_halo(diffusivity, (("col", 0),), SMOOTH)
    for position in range(SMOOTH):
        center = current[:, :, 1:-1]
        kappa_part = kappa_wide[position + 1 : kappa_wide.shape[0] - position - 1]
        current = center + kappa_part[None, None] * (
            current[:, :, 2:] + current[:, :, :-2] + lat_sum(center) - 4.0 * center
        )
    return current


def solution(mesh):
    in_specs = (P("lev", None, "col", None), P("lev", "col", None), P("col", None))
    out_specs = P("lev", None, "col", None)
    return jax.shard_map(
        per_device, mesh=mesh, in_specs=in_specs, out_specs=out_specs, check_vma=False
    )
```

profile of v0, /device:TPU:5, one launch (start us, length us, event | category | flops | bytes accessed | tf_op | source)
XLA Modules:
  0.0 220.1 jit_solution(17643948273532012941)
XLA Ops:
  2.1 2.7 %broadcast.223.clone.2 = f32[3,8,16,24,128]{4,3,2,1,0:T(8,128)} broadcast(f32[]{:T(128)} %constant.259.clone.1), dimensions={} | broadcast | bytes 4718596 | tf_op jit(solution)/shard_map/broadcast.10
  4.8 28.4 %while.120 = (s32[]{:T(128)}, f32[16,24,128]{2,1,0:T(8,128)S(1)}, f32[3,8,16,24,128]{4,3,2,1,0:T(8,128)}, f32[3,8,24,128]{3,2,1,0:T(8,128)S(1)}, f32[3,8,16,24,1...) while((s32[]{:T(128)}, f32[16,24,128]{2,1,0:T(8,128)S(1)}, ...), condition=%wide.region_1.2_spmd.clone, body=%wide.region_0.1_spmd.clone.sunk | while | flops 1695753 | bytes 10003275 | solution.py:54
  34.1 9.4 %all_gather.26 = f32[4,16,24,128]{3,2,1,0:T(8,128)S(1)} all-gather(f32[1,16,24,128]{3,2,1,0:T(8,128)S(1)} %slice.636), channel_id=1, replica_groups=mesh['lev'=4,'col'=8] {'lev'}, dimensions={0}, use_global_device_ids=true | all-gather | bytes 983040 | tf_op jit(solution)/shard_map/all_gather | solution.py:11
  43.6 5.2 %all-gather = f32[96,128]{1,0:T(8,128)S(1)} all-gather(f32[24,128]{1,0:T(8,128)S(1)} %reduce_prod.8), channel_id=2, replica_groups=mesh['lev'=4,'col'=8] {'lev'}, dimensions={0}, use_global_device_ids=true | all-gather | bytes 61440 | tf_op jit(solution)/shard_map/all_gather | solution.py:11
  49.3 5.2 %multiply_add_fusion.3 = f32[3,8,16,24,128]{4,3,2,1,0:T(8,128)} fusion(f32[3,8,16,24,128]{4,3,2,1,0:T(8,128)} %get-tuple-element.717, f32[16,24,128]{2,1,0:T(8,128)S(1)} %get-tuple-element.718, f32[3,8,24,128]{3,2,1,0:T(8,128)S(1)} %bitcast.599), kind=kLoop, calls=%fused_computation.248 | loop fusion | flops 2359296 | bytes 9928704 | tf_op jit(solution)/shard_map/add | solution.py:68
  54.4 2.7 %broadcast.223.clone.1 = f32[3,8,16,24,128]{4,3,2,1,0:T(8,128)} broadcast(f32[]{:T(128)} %constant.259.clone.1), dimensions={} | broadcast | bytes 4718596 | tf_op jit(solution)/shard_map/broadcast.10
  57.1 18.0 %while.122 = (s32[]{:T(128)}, f32[16,24,128]{2,1,0:T(8,128)S(1)}, f32[3,8,16,24,128]{4,3,2,1,0:T(8,128)}, f32[3,8,24,128]{3,2,1,0:T(8,128)S(1)}, f32[3,8,16,24,1...) while((s32[]{:T(128)}, f32[16,24,128]{2,1,0:T(8,128)S(1)}, ...), condition=%wide.region_7.8_spmd.clone, body=%wide.region_6.7_spmd.clone.sunk | while | flops 1695754 | bytes 10002771 | solution.py:54
  76.0 9.8 %all_gather.27 = f32[4,16,24,128]{3,2,1,0:T(8,128)S(1)} all-gather(f32[1,16,24,128]{3,2,1,0:T(8,128)S(1)} %slice.637), channel_id=1, replica_groups=mesh['lev'=4,'col'=8] {'lev'}, dimensions={0}, use_global_device_ids=true | all-gather | bytes 983040 | tf_op jit(solution)/shard_map/all_gather | solution.py:11
  87.6 5.2 %multiply_add_fusion.2 = f32[3,8,16,24,128]{4,3,2,1,0:T(8,128)} fusion(f32[3,8,16,24,128]{4,3,2,1,0:T(8,128)} %get-tuple-element.719, f32[16,24,128]{2,1,0:T(8,128)S(1)} %get-tuple-element.720, f32[3,8,24,128]{3,2,1,0:T(8,128)S(1)} %bitcast.601), kind=kLoop, calls=%fused_computation.247 | loop fusion | flops 2359296 | bytes 9928704 | tf_op jit(solution)/shard_map/add | solution.py:77
  92.8 2.7 %broadcast.223.clone = f32[3,8,16,24,128]{4,3,2,1,0:T(8,128)} broadcast(f32[]{:T(128)} %constant.259.clone.1), dimensions={} | broadcast | bytes 4718596 | tf_op jit(solution)/shard_map/broadcast.10
  95.5 28.4 %while.124 = (s32[]{:T(128)}, f32[16,24,128]{2,1,0:T(8,128)S(1)}, f32[3,8,16,24,128]{4,3,2,1,0:T(8,128)}, f32[3,8,24,128]{3,2,1,0:T(8,128)S(1)}, f32[3,8,16,24,1...) while((s32[]{:T(128)}, f32[16,24,128]{2,1,0:T(8,128)S(1)}, ...), condition=%wide.region_12.13_spmd.clone, body=%wide.region_11.12_spmd.clone.sunk | while | flops 1695753 | bytes 10003275 | solution.py:54
  124.8 7.8 %all_gather.28 = f32[4,16,24,128]{3,2,1,0:T(8,128)S(1)} all-gather(f32[1,16,24,128]{3,2,1,0:T(8,128)S(1)} %slice.638), channel_id=1, replica_groups=mesh['lev'=4,'col'=8] {'lev'}, dimensions={0}, use_global_device_ids=true | all-gather | bytes 983040 | tf_op jit(solution)/shard_map/all_gather | solution.py:11
  133.1 5.2 %multiply_add_fusion.1 = f32[3,8,16,24,128]{4,3,2,1,0:T(8,128)} fusion(f32[3,8,16,24,128]{4,3,2,1,0:T(8,128)} %get-tuple-element.721, f32[16,24,128]{2,1,0:T(8,128)S(1)} %get-tuple-element.722, f32[3,8,24,128]{3,2,1,0:T(8,128)S(1)} %bitcast.600), kind=kLoop, calls=%fused_computation.246 | loop fusion | flops 2359296 | bytes 9928704 | tf_op jit(solution)/shard_map/add | solution.py:68
  138.3 2.7 %broadcast.223 = f32[3,8,16,24,128]{4,3,2,1,0:T(8,128)} broadcast(f32[]{:T(128)} %constant.259.clone.1), dimensions={} | broadcast | bytes 4718596 | tf_op jit(solution)/shard_map/broadcast.10
  141.0 18.0 %while.126 = (s32[]{:T(128)}, f32[16,24,128]{2,1,0:T(8,128)S(1)}, f32[3,8,16,24,128]{4,3,2,1,0:T(8,128)}, f32[3,8,24,128]{3,2,1,0:T(8,128)S(1)}, f32[3,8,16,24,1...) while((s32[]{:T(128)}, f32[16,24,128]{2,1,0:T(8,128)S(1)}, ...), condition=%wide.region_16.17_spmd.clone, body=%wide.region_15.16_spmd.clone.sunk | while | flops 1695754 | bytes 10002771 | solution.py:54
  159.9 9.3 %all_gather.29 = f32[4,16,24,128]{3,2,1,0:T(8,128)S(1)} all-gather(f32[1,16,24,128]{3,2,1,0:T(8,128)S(1)} %slice.639), channel_id=1, replica_groups=mesh['lev'=4,'col'=8] {'lev'}, dimensions={0}, use_global_device_ids=true | all-gather | bytes 983040 | tf_op jit(solution)/shard_map/all_gather | solution.py:11
  169.7 2.9 %multiply_add_fusion = f32[24,16,24,128]{3,2,1,0:T(8,128)S(1)} fusion(f32[16,24,128]{2,1,0:T(8,128)S(1)} %get-tuple-element.724, f32[24,24,128]{2,1,0:T(8,128)S(1)} %rev.10, f32[3,8,16,24,128]{4,3,2,1,0:T(8,128)} %get-tuple-element.723), kind=kLoop, calls=%fused_computation.245 | loop fusion | flops 2359296 | bytes 9928704 | tf_op jit(solution)/shard_map/add | solution.py:77
  173.1 12.9 %collective-permute-start = (f32[24,16,4,128]{3,1,2,0:T(8,128)S(1)}, f32[24,16,4,128]{3,1,2,0:T(8,128)S(1)}, u32[]{:S(2)}, u32[]{:S(2)}) collective-permute-start(f32[24,16,4,128]{3,1,2,0:T(8,128)S(1)} %copy.6), channel_id=1, source_target_pairs={{0,1},{1,2},{2,3},{3,4},{4,5},{5,6},{6,7},{8,9},{9,10},{10,11},{11... | collective-permute-start | bytes 2359304 | tf_op jit(solution)/shard_map/ppermute | solution.py:30
  188.0 3.6 %collective-permute-start.2 = (f32[4,128]{1,0:T(4,128)S(1)}, f32[4,128]{1,0:T(4,128)S(1)}, u32[]{:S(2)}, u32[]{:S(2)}) collective-permute-start(f32[4,128]{1,0:T(4,128)S(1)} %get-tuple-element.1103), channel_id=1, source_target_pairs={{0,1},{1,2},{2,3},{3,4},{4,5},{5,6},{6,7},{8,9},{9,10},{10,11},{11... | collective-permute-start | bytes 6152 | tf_op jit(solution)/shard_map/ppermute | solution.py:30
  194.9 4.5 %collective-permute-done.3 = f32[4,128]{1,0:T(4,128)S(1)} collective-permute-done((f32[4,128]{1,0:T(4,128)S(1)}, f32[4,128]{1,0:T(4,128)S(1)}, u32[]{:S(2)}, u32[]{:S(2)}) %collective-permute-start.3) | collective-permute-done | bytes 2080 | tf_op jit(solution)/shard_map/ppermute | solution.py:33
  202.4 3.4 %fusion.72 = f32[24,16,30,128]{3,2,1,0:T(8,128)S(1)} fusion(f32[24,16,30,128]{3,2,1,0:T(8,128)S(1)} %slice.642, f32[24,16,32,128]{3,2,1,0:T(8,128)S(1)} %pad_maximum_fusion, f32[30,128]{1,0:T(8,128)S(1)} %slice.643), kind=kLoop, calls=%fused_computation.224 | loop fusion | flops 10321920 | bytes 23608320 | tf_op jit(solution)/shard_map/add | solution.py:95
  207.0 3.4 %fusion.77 = f32[24,16,28,128]{3,2,1,0:T(8,128)S(1)} fusion(f32[24,16,28,128]{3,2,1,0:T(8,128)S(1)} %slice.646, f32[24,16,30,128]{3,2,1,0:T(8,128)S(1)} %fusion.72, f32[28,128]{1,0:T(8,128)S(1)} %slice.647), kind=kLoop, calls=%fused_computation.229 | loop fusion | flops 9633792 | bytes 22034432 | tf_op jit(solution)/shard_map/add | solution.py:95
  211.6 3.4 %fusion.82 = f32[24,16,26,128]{3,2,1,0:T(8,128)S(1)} fusion(f32[24,16,26,128]{3,2,1,0:T(8,128)S(1)} %slice.650, f32[24,16,28,128]{3,2,1,0:T(8,128)S(1)} %fusion.77, f32[26,128]{1,0:T(8,128)S(1)} %slice.651), kind=kLoop, calls=%fused_computation.234 | loop fusion | flops 8945664 | bytes 20460544 | tf_op jit(solution)/shard_map/add | solution.py:95
  215.8 4.3 %fusion.87 = f32[24,16,24,128]{3,2,1,0:T(8,128)} fusion(f32[24,16,24,128]{3,2,1,0:T(8,128)S(1)} %slice.654, f32[24,16,26,128]{3,2,1,0:T(8,128)S(1)} %fusion.82, f32[24,128]{1,0:T(8,128)S(1)} %copy-done.1), kind=kLoop, calls=%fused_computation.243 | loop fusion | flops 8257536 | bytes 18886656 | tf_op jit(solution)/shard_map/add | solution.py:95
  (197 shorter events, 114.4 us)
Async XLA Ops:
  0.0 4.8 %copy-start = (f32[24,24,128]{2,1,0:T(8,128)S(1)}, f32[24,24,128]{2,1,0:T(8,128)}, u32[]{:S(2)}) copy-start(f32[24,24,128]{2,1,0:T(8,128)} %param.20) | copy-start | bytes 884740
  172.5 15.4 %copy-start.1 = (f32[24,128]{1,0:T(8,128)S(1)}, f32[24,128]{1,0:T(8,128)}, u32[]{:S(2)}) copy-start(f32[24,128]{1,0:T(8,128)} %param.21) | copy-start | bytes 36868
  173.1 26.3 %collective-permute-start = (f32[24,16,4,128]{3,1,2,0:T(8,128)S(1)}, f32[24,16,4,128]{3,1,2,0:T(8,128)S(1)}, u32[]{:S(2)}, u32[]{:S(2)}) collective-permute-start(f32[24,16,4,128]{3,1,2,0:T(8,128)S(1)} %copy.6), channel_id=1, source_target_pairs={{0,1},{1,2},{2,3},{3,4},{4,5},{5,6},{6,7},{8,9},{9,10},{10,11},{11... | collective-permute-start | bytes 2359304 | tf_op jit(solution)/shard_map/ppermute | solution.py:30
  186.0 13.7 %collective-permute-start.1 = (f32[24,16,4,128]{3,1,2,0:T(8,128)S(1)}, f32[24,16,4,128]{3,1,2,0:T(8,128)S(1)}, u32[]{:S(2)}, u32[]{:S(2)}) collective-permute-start(f32[24,16,4,128]{3,1,2,0:T(8,128)S(1)} %copy.7), channel_id=1, source_target_pairs={{1,0},{2,1},{3,2},{4,3},{5,4},{6,5},{7,6},{9,8},{10,9},{11,10},{12... | collective-permute-start | bytes 2359304 | tf_op jit(solution)/shard_map/ppermute | solution.py:33
  188.0 6.9 %collective-permute-start.2 = (f32[4,128]{1,0:T(4,128)S(1)}, f32[4,128]{1,0:T(4,128)S(1)}, u32[]{:S(2)}, u32[]{:S(2)}) collective-permute-start(f32[4,128]{1,0:T(4,128)S(1)} %get-tuple-element.1103), channel_id=1, source_target_pairs={{0,1},{1,2},{2,3},{3,4},{4,5},{5,6},{6,7},{8,9},{9,10},{10,11},{11... | collective-permute-start | bytes 6152 | tf_op jit(solution)/shard_map/ppermute | solution.py:30
  191.6 7.7 %collective-permute-start.3 = (f32[4,128]{1,0:T(4,128)S(1)}, f32[4,128]{1,0:T(4,128)S(1)}, u32[]{:S(2)}, u32[]{:S(2)}) collective-permute-start(f32[4,128]{1,0:T(4,128)S(1)} %get-tuple-element.1104), channel_id=1, source_target_pairs={{1,0},{2,1},{3,2},{4,3},{5,4},{6,5},{7,6},{9,8},{10,9},{11,10},{12... | collective-permute-start | bytes 6152 | tf_op jit(solution)/shard_map/ppermute | solution.py:33
where the time goes:
time: 224 us; the launch traced here: 220 us
  other arithmetic  114 us (51%)
  blocking collectives  41.6 us (19%)
  local copies, waits for them, and re-layouts  36.8 us (16%)
  starting transfers between devices  20.5 us (9%)
  waiting for transfers between devices  5.63 us (3%)
    while x66, other arithmetic  70.6 us
    all_gather x5, blocking collectives, entering_2(): everything = jax.tree.map(lambda part: lax.all_gather(part, axis), x)  41.6 us
    ppermute x2, starting transfers between devices, with_halo(): lax.ppermute(lax.slice_in_dim(block, block.shape[dim] - width, None, axis...  16.5 us
    dynamic_update_slice x12, local copies, waits for them, and re-layouts, sweep_levels(): lax.scan(run_block, start, (rate_blocks, field_blocks), reverse=backward)  15.2 us
    add x4, other arithmetic, per_device(): center + kappa_part[None, None] * (current[:, :, 2:] + current[:, :, :-2]...  14.6 us
    another operation x4, local copies, waits for them, and re-layouts  10.9 us
    add x2, other arithmetic, forward_pass(): return within + growth[:, None] * entering[1][None]  10.3 us
    add x2, other arithmetic, backward_pass(): return within + growth[:, None] * entering[1][None]  8.02 us
  transfers between devices with their start and end apart: 4, of which 2 were waited for; matrix products, arithmetic and copies ran while one was open for 0% of the time, Pallas kernels for 0%

commit v1 on v0

v1 whole, which is shorter than its diff:
```python
import functools
import jax
import jax.numpy as jnp
from jax import lax
from jax.experimental import pallas as pl
from jax.experimental.pallas import tpu as pltpu
from jax.sharding import PartitionSpec as P

SMOOTH = 4
MESH = pl.DeviceIdType.MESH
F32 = jnp.float32


def exchange_kernel(
    n, nc, x_hbm, w_ref, kappa_ref,
    xh_out, wh_out, kh_out, e_out, eh_out,
    xv, work, sums, coef, gathered, solved, entering,
    load_sem, coef_send, coef_recv, sum_send, sum_recv, back_send, back_recv,
    halo_send, halo_recv, edge_send, edge_recv, out_sem,
):
    levels, members, cols, lanes = xv.shape
    share = members // n
    me = lax.axis_index("lev")
    col = lax.axis_index("col")
    has_low = col > 0
    has_high = col < nc - 1
    groups = cols // 8

    load = pltpu.make_async_copy(x_hbm, xv, load_sem)
    load.start()

    barrier = pltpu.get_barrier_semaphore()
    for j in range(1, n):
        pl.semaphore_signal(barrier, inc=1, device_id={"lev": lax.rem(me + j, n)}, device_id_type=MESH)
    for step in (1, nc - 1):
        pl.semaphore_signal(barrier, inc=1, device_id={"col": lax.rem(col + step, nc)}, device_id_type=MESH)
    pl.semaphore_wait(barrier, n + 1)

    def to_high(src, dst, sem):
        return pltpu.make_async_remote_copy(
            src_ref=src, dst_ref=dst, send_sem=halo_send.at[sem], recv_sem=halo_recv.at[sem],
            device_id={"col": lax.rem(col + 1, nc)}, device_id_type=MESH)

    def to_low(src, dst, sem):
        return pltpu.make_async_remote_copy(
            src_ref=src, dst_ref=dst, send_sem=halo_send.at[sem], recv_sem=halo_recv.at[sem],
            device_id={"col": lax.rem(col + nc - 1, nc)}, device_id_type=MESH)

    s = SMOOTH
    up_copies = [
        to_high(x_hbm.at[:, :, pl.ds(cols - s, s)], xh_out.at[:, :, pl.ds(s, s)], 0),
        to_high(w_ref.at[:, pl.ds(cols - s, s)], wh_out.at[:, pl.ds(s, s)], 1),
        to_high(kappa_ref.at[pl.ds(cols - s, s)], kh_out.at[pl.ds(s, s)], 2),
    ]
    down_copies = [
        to_low(x_hbm.at[:, :, pl.ds(0, s)], xh_out.at[:, :, pl.ds(0, s)], 3),
        to_low(w_ref.at[:, pl.ds(0, s)], wh_out.at[:, pl.ds(0, s)], 4),
        to_low(kappa_ref.at[pl.ds(0, s)], kh_out.at[pl.ds(0, s)], 5),
    ]

    @pl.when(has_high)
    def _():
        for copy in up_copies:
            copy.start()

    @pl.when(has_low)
    def _():
        for copy in down_copies:
            copy.start()

    def coefficients(g, carry):
        rows = pl.ds(pl.multiple_of(g * 8, 8), 8)
        w = [w_ref[k, rows] for k in range(levels)]
        f1 = jnp.ones((8, lanes), F32)
        up = []
        for k in range(levels):
            f1 = w[k] * f1
            up.append(f1)
        alpha = f1
        a = jnp.zeros((8, lanes), F32)
        b = jnp.ones((8, lanes), F32)
        da, db = [None] * levels, [None] * levels
        for k in reversed(range(levels)):
            a = w[k] * a + (1.0 - w[k]) * up[k]
            b = w[k] * b
            da[k], db[k] = a, b
        beta = a
        a = jnp.zeros((8, lanes), F32)
        b = jnp.zeros((8, lanes), F32)
        for k in range(levels):
            a = w[k] * a + (1.0 - w[k]) * da[k]
            b = w[k] * b + (1.0 - w[k]) * db[k]
            da[k], db[k] = a, b
        delta, gamma = a, b
        a = jnp.zeros((8, lanes), F32)
        b = jnp.zeros((8, lanes), F32)
        for k in reversed(range(levels)):
            a = w[k] * a + (1.0 - w[k]) * da[k]
            b = w[k] * b + (1.0 - w[k]) * db[k]
        for i, value in enumerate((alpha, beta, gamma, delta, b, a)):
            coef[me, i, rows] = value
        return carry

    lax.fori_loop(0, groups, coefficients, 0)
    coef_copies = []
    for j in range(1, n):
        copy = pltpu.make_async_remote_copy(
            src_ref=coef.at[me], dst_ref=coef.at[me], send_sem=coef_send.at[j], recv_sem=coef_recv.at[j],
            device_id={"lev": lax.rem(me + j, n)}, device_id_type=MESH)
        copy.start()
        coef_copies.append(copy)

    load.wait()
    mb = 8

    def local(t, carry):
        g = lax.rem(t, groups)
        rows = pl.ds(pl.multiple_of(g * 8, 8), 8)
        mem = pl.ds((t // groups) * mb, mb)
        state = jnp.zeros((mb, 8, lanes), F32)
        for k in range(levels):
            w = w_ref[k, rows][None]
            state = w * state + (1.0 - w) * xv[k, mem, rows]
            work[k] = state
        sums[0, mem, rows] = state
        state = jnp.zeros((mb, 8, lanes), F32)
        for k in reversed(range(levels)):
            w = w_ref[k, rows][None]
            state = w * state + (1.0 - w) * work[k]
            work[k] = state
        sums[2, mem, rows] = state
        state = jnp.zeros((mb, 8, lanes), F32)
        for k in range(levels):
            w = w_ref[k, rows][None]
            state = w * state + (1.0 - w) * work[k]
            work[k] = state
        sums[1, mem, rows] = state
        state = jnp.zeros((mb, 8, lanes), F32)
        for k in reversed(range(levels)):
            w = w_ref[k, rows][None]
            state = w * state + (1.0 - w) * work[k]
        sums[3, mem, rows] = state
        return carry

    lax.fori_loop(0, groups * (members // mb), local, 0)

    def half(kind):
        return pl.ds(2 * kind, 2)

    def gives(kind, dev):
        return dev < n - 1 if kind == 0 else dev > 0

    def takes(kind, dev):
        return dev > 0 if kind == 0 else dev < n - 1

    def sum_copy(j, kind):
        peer = lax.rem(me + j, n)
        return pltpu.make_async_remote_copy(
            src_ref=sums.at[half(kind), pl.ds(peer * share, share)], dst_ref=gathered.at[me, half(kind)],
            send_sem=sum_send.at[j, kind], recv_sem=sum_recv.at[j, kind],
            device_id={"lev": peer}, device_id_type=MESH)

    for j in range(1, n):
        for kind in range(2):
            @pl.when(gives(kind, me))
            def _(j=j, kind=kind):
                sum_copy(j, kind).start()

    gathered[me] = sums[:, pl.ds(me * share, share)]
    for j in range(1, n):
        coef_copies[j - 1].wait_recv()
    for j in range(1, n):
        source = lax.rem(me + n - j, n)
        for kind in range(2):
            @pl.when(gives(kind, source))
            def _(j=j, kind=kind):
                sum_copy(j, kind).wait_recv()

    def solve(t, carry):
        g = lax.rem(t, groups)
        rows = pl.ds(pl.multiple_of(g * 8, 8), 8)
        m = t // groups

        def c(d, i):
            return coef[d, i, rows]

        zero = jnp.zeros((8, lanes), F32)
        f1 = [zero]
        for d in range(n - 1):
            f1.append(c(d, 0) * f1[d] + gathered[d, 0, m, rows])
        b1 = [zero] * n
        for d in range(n - 1, 0, -1):
            b1[d - 1] = c(d, 0) * b1[d] + c(d, 1) * f1[d] + gathered[d, 2, m, rows]
        f2 = [zero]
        for d in range(n - 1):
            f2.append(c(d, 0) * f2[d] + c(d, 2) * b1[d] + c(d, 3) * f1[d] + gathered[d, 1, m, rows])
        b2 = [zero] * n
        for d in range(n - 1, 0, -1):
            b2[d - 1] = (c(d, 0) * b2[d] + c(d, 1) * f2[d] + c(d, 4) * b1[d] + c(d, 5) * f1[d]
                         + gathered[d, 3, m, rows])
        for d in range(n):
            for i, value in enumerate((f1[d], f2[d], b1[d], b2[d])):
                solved[d, i, m, rows] = value
        return carry

    lax.fori_loop(0, groups * share, solve, 0)

    def back_copy(j, kind):
        peer = lax.rem(me + j, n)
        return pltpu.make_async_remote_copy(
            src_ref=solved.at[peer, half(kind)], dst_ref=entering.at[half(kind), pl.ds(me * share, share)],
            send_sem=back_send.at[j, kind], recv_sem=back_recv.at[j, kind],
            device_id={"lev": peer}, device_id_type=MESH)

    for j in range(1, n):
        peer = lax.rem(me + j, n)
        for kind in range(2):
            @pl.when(takes(kind, peer))
            def _(j=j, kind=kind):
                back_copy(j, kind).start()

    entering[:, pl.ds(me * share, share)] = solved[me]

    for kind in range(2):
        @pl.when(takes(kind, me) == False)
        def _(kind=kind):
            for j in range(1, n):
                entering[half(kind), pl.ds(lax.rem(me + j, n) * share, share)] = jnp.zeros(
                    (2, share, cols, lanes), F32)

        @pl.when(takes(kind, me))
        def _(kind=kind):
            for j in range(1, n):
                back_copy(j, kind).wait_recv()

    out = pltpu.make_async_copy(entering, e_out, out_sem)
    out.start()
    edge_high = pltpu.make_async_remote_copy(
        src_ref=entering.at[:, :, pl.ds(cols - s, s)], dst_ref=eh_out.at[:, :, pl.ds(s, s)],
        send_sem=edge_send.at[0], recv_sem=edge_recv.at[0],
        device_id={"col": lax.rem(col + 1, nc)}, device_id_type=MESH)
    edge_low = pltpu.make_async_remote_copy(
        src_ref=entering.at[:, :, pl.ds(0, s)], dst_ref=eh_out.at[:, :, pl.ds(0, s)],
        send_sem=edge_send.at[1], recv_sem=edge_recv.at[1],
        device_id={"col": lax.rem(col + nc - 1, nc)}, device_id_type=MESH)

    @pl.when(has_high)
    def _():
        edge_high.start()

    @pl.when(has_low)
    def _():
        edge_low.start()

    for j in range(1, n):
        coef_copies[j - 1].wait_send()
        for kind in range(2):
            @pl.when(gives(kind, me))
            def _(j=j, kind=kind):
                sum_copy(j, kind).wait_send()

            @pl.when(takes(kind, lax.rem(me + j, n)))
            def _(j=j, kind=kind):
                back_copy(j, kind).wait_send()

    @pl.when(has_high)
    def _():
        for copy in up_copies + [edge_high]:
            copy.wait_send()
        for copy in down_copies + [edge_low]:
            copy.wait_recv()

    @pl.when(has_low)
    def _():
        for copy in down_copies + [edge_low]:
            copy.wait_send()
        for copy in up_copies + [edge_high]:
            copy.wait_recv()

    out.wait()


def exchange(n, nc, x, w, kappa):
    levels, members, cols, lanes = x.shape
    share = members // n
    s2 = 2 * SMOOTH
    hbm = pl.BlockSpec(memory_space=pl.ANY)
    vmem = pl.BlockSpec(memory_space=pltpu.VMEM)
    dma = pltpu.SemaphoreType.DMA
    return pl.pallas_call(
        functools.partial(exchange_kernel, n, nc),
        out_shape=[
            jax.ShapeDtypeStruct((levels, members, s2, lanes), F32),
            jax.ShapeDtypeStruct((levels, s2, lanes), F32),
            jax.ShapeDtypeStruct((s2, lanes), F32),
            jax.ShapeDtypeStruct((4, members, cols, lanes), F32),
            jax.ShapeDtypeStruct((4, members, s2, lanes), F32),
        ],
        in_specs=[hbm, vmem, vmem],
        out_specs=[hbm] * 5,
        scratch_shapes=[
            pltpu.VMEM(x.shape, F32),
            pltpu.VMEM((levels, 8, 8, lanes), F32),
            pltpu.VMEM((4, members, cols, lanes), F32),
            pltpu.VMEM((n, 6, cols, lanes), F32),
            pltpu.VMEM((n, 4, share, cols, lanes), F32),
            pltpu.VMEM((n, 4, share, cols, lanes), F32),
            pltpu.VMEM((4, members, cols, lanes), F32),
            dma, dma((n,)), dma((n,)), dma((n, 2)), dma((n, 2)), dma((n, 2)), dma((n, 2)),
            dma((6,)), dma((6,)), dma((2,)), dma((2,)), dma,
        ],
        compiler_params=pltpu.CompilerParams(
            collective_id=0, has_side_effects=True, vmem_limit_bytes=40 << 20),
        name="exchange",
    )(x, w, kappa)


def finish_kernel(nc, x_ref, xh_ref, w_ref, wh_ref, k_ref, kh_ref, e_ref, eh_ref, out_ref, u_ref, wall, kall):
    levels, mb, cols, lanes = x_ref.shape
    col = lax.axis_index("col")
    wide = cols + 8
    sub = lax.broadcasted_iota(jnp.int32, (8, lanes), 0)
    first = jnp.where(col < nc - 1, 0, SMOOTH)
    last = jnp.where(col > 0, 2 * SMOOTH, SMOOTH)
    real = (sub >= first) & (sub < last)

    @pl.when(pl.program_id(0) == 0)
    def _():
        wall[:, :cols] = w_ref[...]
        wall[:, cols:] = jnp.where(real[None], wh_ref[...], 0.5)
        kall[:cols] = k_ref[...]
        kall[cols:] = jnp.where(real, kh_ref[...], 0.0)

    def columns(rows, xs, f1, f2, b1, b2):
        state = f1
        for k in range(levels):
            w = wall[k, rows][None]
            state = w * state + (1.0 - w) * xs(k)
            u_ref[k, :, rows] = state
        for state, order in ((b1, range(levels - 1, -1, -1)), (f2, range(levels)), (b2, range(levels - 1, -1, -1))):
            for k in order:
                w = wall[k, rows][None]
                state = w * state + (1.0 - w) * u_ref[k, :, rows]
                u_ref[k, :, rows] = state

    for g in range(cols // 8):
        rows = pl.ds(g * 8, 8)
        columns(rows, lambda k: x_ref[k, :, rows], *(e_ref[i, :, rows] for i in range(4)))
    keep = real[None]
    columns(pl.ds(cols, 8), lambda k: jnp.where(keep, xh_ref[k], 0.0),
            *(jnp.where(keep, eh_ref[i], 0.0) for i in range(4)))

    lane = lax.broadcasted_iota(jnp.int32, (wide, lanes), 1)
    kappa = kall[...]
    middle = (1.0 - 4.0 * kappa)[None]
    south = jnp.where(lane > 0, kappa, 0.0)[None]
    north = jnp.where(lane < lanes - 1, kappa, 0.0)[None]
    kappa = kappa[None]

    def diffuse(k, carry):
        u = u_ref[k]
        for step in range(SMOOTH):
            u = (middle * u + kappa * (pltpu.roll(u, 1, 1) + pltpu.roll(u, wide - 1, 1))
                 + south * pltpu.roll(u, 1, 2) + north * pltpu.roll(u, lanes - 1, 2))
        out_ref[k] = u[:, :cols]
        return carry

    lax.fori_loop(0, levels, diffuse, 0)


def finish(nc, x, xh, w, wh, kappa, kh, e, eh):
    levels, members, cols, lanes = x.shape
    mb = 2

    def by_member(shape):
        return pl.BlockSpec((shape[0], mb) + shape[2:], lambda i: (0, i, 0, 0))

    def whole(shape):
        return pl.BlockSpec(shape, lambda i: (0,) * len(shape))

    return pl.pallas_call(
        functools.partial(finish_kernel, nc),
        grid=(members // mb,),
        out_shape=jax.ShapeDtypeStruct(x.shape, F32),
        in_specs=[by_member(x.shape), by_member(xh.shape), whole(w.shape), whole(wh.shape),
                  whole(kappa.shape), whole(kh.shape), by_member(e.shape), by_member(eh.shape)],
        out_specs=by_member(x.shape),
        scratch_shapes=[
            pltpu.VMEM((levels, mb, cols + 8, lanes), F32),
            pltpu.VMEM((levels, cols + 8, lanes), F32),
            pltpu.VMEM((cols + 8, lanes), F32),
        ],
        compiler_params=pltpu.CompilerParams(vmem_limit_bytes=40 << 20),
        name="finish",
    )(x, xh, w, wh, kappa, kh, e, eh)


def solution(mesh):
    n, nc = mesh.shape["lev"], mesh.shape["col"]

    def per_device(x, w, kappa):
        xh, wh, kh, e, eh = exchange(n, nc, x, w, kappa)
        return finish(nc, x, xh, w, wh, kappa, kh, e, eh)

    in_specs = (P("lev", None, "col", None), P("lev", "col", None), P("col", None))
    out_specs = P("lev", None, "col", None)
    return jax.shard_map(per_device, mesh=mesh, in_specs=in_specs, out_specs=out_specs, check_vma=False)
```

time: 224 us -> 101 us (0.45); the launches traced: 220 us -> 101 us
  other arithmetic: 114 us -> 0 us
  Pallas kernels: 0 us -> 96.5 us
  blocking collectives: 41.6 us -> 0 us
  local copies, waits for them, and re-layouts: 36.8 us -> 4 us
  starting transfers between devices: 20.5 us -> 0 us
  waiting for transfers between devices: 5.63 us -> 0 us
    pallas_call x0 -> x2, Pallas kernels: none -> 96.5 us  [the longest x1 64.8 us: finish(): pl.pallas_call(functools.partial(finish_kernel, nc), grid=(members // mb,...]
    while x66 -> x0, other arithmetic: 70.6 us -> none
    all_gather x5 -> x0, blocking collectives: 41.6 us -> none  [entering_2(): everything = jax.tree.map(lambda part: lax.all_gather(part, axis), x)]
    add x8 -> x0, other arithmetic: 32.9 us -> none  [the longest x4 14.6 us: per_device(): center + kappa_part[None, None] * (current[:, :, 2:] + current[:, :, :-2]...]
    ppermute x4 -> x0, starting transfers between devices: 20.5 us -> none  [the longest x2 16.5 us: with_halo(): lax.ppermute(lax.slice_in_dim(block, block.shape[dim] - width, None, axis...]
    dynamic_update_slice x12 -> x0, local copies, waits for them, and re-layouts: 15.2 us -> none  [sweep_levels(): lax.scan(run_block, start, (rate_blocks, field_blocks), reverse=backward)]
    another operation x10 -> x0, local copies, waits for them, and re-layouts: 11 us -> none
    slice x15 -> x0, local copies, waits for them, and re-layouts: 8.64 us -> none  [the longest x4 4.29 us: per_device(): center = current[:, :, 1:-1]]
  transfers between devices with their start and end apart: 4 -> 0, of which waited for: 2 -> 0; matrix products, arithmetic and copies ran while one was open for 0% -> 0% of each run, Pallas kernels for 0% -> 0%
where the time goes in v1:
time: 101 us
  Pallas kernels  96.5 us (96%)
  local copies, waits for them, and re-layouts  4 us (4%)
    pallas_call x1, Pallas kernels, finish(): pl.pallas_call(functools.partial(finish_kernel, nc), grid=(members // mb,...  64.8 us
    pallas_call x1, Pallas kernels, exchange(): pl.pallas_call(functools.partial(exchange_kernel, n, nc), out_shape=[jax....  31.7 us
    unnamed x6, local copies, waits for them, and re-layouts  4 us

profile of v1, /device:TPU:5, one launch (start us, length us, event | category | flops | bytes accessed | tf_op | source)
XLA Modules:
  0.0 100.5 jit_solution(15882787125547649235)
XLA Ops:
  0.0 0.0 copy-start
  0.0 2.3 %copy-done = f32[24,16,24,128]{3,2,1,0:T(8,128)S(1)} copy-done((f32[24,16,24,128]{3,2,1,0:T(8,128)S(1)}, f32[24,16,24,128]{3,2,1,0:T(8,128)}, u32[]{:S(2)}) %copy-start) | copy-done | bytes 4718616
  2.3 0.0 copy-start.1
  2.3 1.0 copy-done.1
  3.3 0.0 copy-start.2
  3.3 0.7 copy-done.2
  4.0 31.7 %exchange.1 = (f32[24,16,8,128]{3,2,1,0:T(8,128)S(1)}, f32[24,8,128]{2,1,0:T(8,128)S(1)}, f32[8,128]{1,0:T(8,128)S(1)}, f32[4,16,24,128]{3,2,1,0:T(8,128)S(1)}, f32[4,16,8,128]{3,2,1,0:T(8,128)S(1)}) custom-call(f32[24,16,24,128]{3,2,1,0:T(8,128)S(1)} %copy-done, f32[24,24,128]{2,1,0:T(8,128)S(1)} %copy-done.1, f32[24,128]{1,0:T(8,128)S(1)} %copy-done.2), custom_call_target="tpu_custom_call" | custom-call | tf_op jit(solution)/shard_map/exchange/pallas_call | solution.py:290
  35.7 64.8 %finish.1 = f32[24,16,24,128]{3,2,1,0:T(8,128)} custom-call(f32[24,16,24,128]{3,2,1,0:T(8,128)S(1)} %copy-done, f32[24,16,8,128]{3,2,1,0:T(8,128)S(1)} %get-tuple-element.10.xh_ref, f32[24,24,128]{2,1,0:T(8,128)S(1)} %copy-done.1, f32[24,8,128]{2,1,0:T(8,128)S(1)} %get-tuple-element.11.wh_ref, f32[24,128]{1,0:T(8,128)S(1)} %copy-done.2, ...), custom_call_target="tpu_custom_call" | custom-call | tf_op jit(solution)/shard_map/finish/pallas_call | solution.py:381
Async XLA Ops:
  0.0 2.3 %copy-start = (f32[24,16,24,128]{3,2,1,0:T(8,128)S(1)}, f32[24,16,24,128]{3,2,1,0:T(8,128)}, u32[]{:S(2)}) copy-start(f32[24,16,24,128]{3,2,1,0:T(8,128)} %x_ref.1) | copy-start | bytes 14155780
  2.3 1.0 copy-start.1
  3.3 0.7 copy-start.2

commit v2 on v1

--- a/solution.py
+++ b/solution.py
@@ -296,7 +296,7 @@
             jax.ShapeDtypeStruct((4, members, cols, lanes), F32),
             jax.ShapeDtypeStruct((4, members, s2, lanes), F32),
         ],
-        in_specs=[hbm, vmem, vmem],
+        in_specs=[pl.BlockSpec(memory_space=pltpu.HBM), vmem, vmem],
         out_specs=[hbm] * 5,
         scratch_shapes=[
             pltpu.VMEM(x.shape, F32),
@@ -315,62 +315,86 @@
     )(x, w, kappa)
 
 
-def finish_kernel(nc, x_ref, xh_ref, w_ref, wh_ref, k_ref, kh_ref, e_ref, eh_ref, out_ref, u_ref, wall, kall):
+def finish_kernel(nc, x_ref, xh_ref, w_ref, wh_ref, k_ref, kh_ref, e_ref, eh_ref, out_ref, a_ref, b_ref, wall, kall):
     levels, mb, cols, lanes = x_ref.shape
     col = lax.axis_index("col")
-    wide = cols + 8
     sub = lax.broadcasted_iota(jnp.int32, (8, lanes), 0)
     first = jnp.where(col < nc - 1, 0, SMOOTH)
     last = jnp.where(col > 0, 2 * SMOOTH, SMOOTH)
     real = (sub >= first) & (sub < last)
+    low, main, high = 8, 16, 16 + cols
 
     @pl.when(pl.program_id(0) == 0)
     def _():
         wall[:, :cols] = w_ref[...]
         wall[:, cols:] = jnp.where(real[None], wh_ref[...], 0.5)
-        kall[:cols] = k_ref[...]
-        kall[cols:] = jnp.where(real, kh_ref[...], 0.0)
-
-    def columns(rows, xs, f1, f2, b1, b2):
-        state = f1
-        for k in range(levels):
-            w = wall[k, rows][None]
-            state = w * state + (1.0 - w) * xs(k)
-            u_ref[k, :, rows] = state
-        for state, order in ((b1, range(levels - 1, -1, -1)), (f2, range(levels)), (b2, range(levels - 1, -1, -1))):
-            for k in order:
-                w = wall[k, rows][None]
-                state = w * state + (1.0 - w) * u_ref[k, :, rows]
-                u_ref[k, :, rows] = state
-
-    for g in range(cols // 8):
-        rows = pl.ds(g * 8, 8)
-        columns(rows, lambda k: x_ref[k, :, rows], *(e_ref[i, :, rows] for i in range(4)))
+        lane = lax.broadcasted_iota(jnp.int32, (cols + 8, lanes), 1)
+        kappa = jnp.concatenate([k_ref[...], jnp.where(real, kh_ref[...], 0.0)], axis=0)
+        kall[0] = kappa
+        kall[1] = 1.0 - 4.0 * kappa
+        kall[2] = jnp.where(lane > 0, kappa, 0.0)
+        kall[3] = jnp.where(lane < lanes - 1, kappa, 0.0)
+
     keep = real[None]
-    columns(pl.ds(cols, 8), lambda k: jnp.where(keep, xh_ref[k], 0.0),
-            *(jnp.where(keep, eh_ref[i], 0.0) for i in range(4)))
-
-    lane = lax.broadcasted_iota(jnp.int32, (wide, lanes), 1)
-    kappa = kall[...]
-    middle = (1.0 - 4.0 * kappa)[None]
-    south = jnp.where(lane > 0, kappa, 0.0)[None]
-    north = jnp.where(lane < lanes - 1, kappa, 0.0)[None]
-    kappa = kappa[None]
-
-    def diffuse(k, carry):
-        u = u_ref[k]
-        for step in range(SMOOTH):
-            u = (middle * u + kappa * (pltpu.roll(u, 1, 1) + pltpu.roll(u, wide - 1, 1))
-                 + south * pltpu.roll(u, 1, 2) + north * pltpu.roll(u, lanes - 1, 2))
-        out_ref[k] = u[:, :cols]
-        return carry
-
-    lax.fori_loop(0, levels, diffuse, 0)
+
+    def start(i):
+        return jnp.concatenate([e_ref[i], jnp.where(keep, eh_ref[i], 0.0)], axis=1)
+
+    span = pl.ds(main, cols + 8)
+    state = start(0)
+    for k in range(levels):
+        w = wall[k][None]
+        x = jnp.concatenate([x_ref[k], jnp.where(keep, xh_ref[k], 0.0)], axis=1)
+        state = w * state + (1.0 - w) * x
+        a_ref[k, :, span] = state
+    for i in (2, 1, 3):
+        state = start(i)
+        for k in range(levels) if i == 1 else reversed(range(levels)):
+            w = wall[k][None]
+            state = w * state + (1.0 - w) * a_ref[k, :, span]
+            a_ref[k, :, span] = state
+            if i == 3:
+                a_ref[k, :, pl.ds(low, 8)] = state[:, cols:]
+
+    upper = sub < SMOOTH
+
+    chunk = max(c for c in range(1, 9) if levels % c == 0)
+
+    def tile(src, k, m, at, rows, east, west):
+        u = src[k, m, pl.ds(at, 8)]
+        return (kall[1, rows] * u + kall[0, rows] * (east + west)
+                + kall[2, rows] * pltpu.roll(u, 1, 1) + kall[3, rows] * pltpu.roll(u, lanes - 1, 1))
+
+    for step in range(SMOOTH):
+        src, dst = (a_ref, b_ref) if step % 2 == 0 else (b_ref, a_ref)
+        final = step == SMOOTH - 1
+
+        def body(c, carry, src=src, dst=dst, final=final):
+            for dk in range(chunk):
+                k = c * chunk + dk
+                for m in range(mb):
+                    for g in range(cols // 8):
+                        at = main + 8 * g
+                        rows = pl.ds(8 * g, 8)
+                        value = tile(src, k, m, at, rows, src[k, m, pl.ds(at + 1, 8)], src[k, m, pl.ds(at - 1, 8)])
+                        if final:
+                            out_ref[k, m, rows] = value
+                        else:
+                            dst[k, m, pl.ds(at, 8)] = value
+                    if not final:
+                        east = jnp.where(upper, src[k, m, pl.ds(high + 1, 8)], src[k, m, pl.ds(low + 1, 8)])
+                        west = jnp.where(upper, src[k, m, pl.ds(high - 1, 8)], src[k, m, pl.ds(low - 1, 8)])
+                        value = tile(src, k, m, high, pl.ds(cols, 8), east, west)
+                        dst[k, m, pl.ds(high, 8)] = value
+                        dst[k, m, pl.ds(low, 8)] = value
+            return carry
+
+        lax.fori_loop(0, levels // chunk, body, 0)
 
 
 def finish(nc, x, xh, w, wh, kappa, kh, e, eh):
     levels, members, cols, lanes = x.shape
-    mb = 2
+    mb = 4
 
     def by_member(shape):
         return pl.BlockSpec((shape[0], mb) + shape[2:], lambda i: (0, i, 0, 0))
@@ -386,9 +410,10 @@
                   whole(kappa.shape), whole(kh.shape), by_member(e.shape), by_member(eh.shape)],
         out_specs=by_member(x.shape),
         scratch_shapes=[
-            pltpu.VMEM((levels, mb, cols + 8, lanes), F32),
+            pltpu.VMEM((levels, mb, cols + 32, lanes), F32),
+            pltpu.VMEM((levels, mb, cols + 32, lanes), F32),
             pltpu.VMEM((levels, cols + 8, lanes), F32),
-            pltpu.VMEM((cols + 8, lanes), F32),
+            pltpu.VMEM((4, cols + 8, lanes), F32),
         ],
         compiler_params=pltpu.CompilerParams(vmem_limit_bytes=40 << 20),
         name="finish",

time: 101 us -> 56.1 us (0.56)
  Pallas kernels: 96.5 us -> 51.8 us
    pallas_call x1, Pallas kernels: 64.8 us -> 20.1 us  [finish(): pl.pallas_call(functools.partial(finish_kernel, nc), grid=(members // mb,...]
where the time goes in v2:
time: 56.1 us; the launch traced here: 55.8 us
  Pallas kernels  51.8 us (92%)
  local copies, waits for them, and re-layouts  4 us (7%)
    pallas_call x1, Pallas kernels, exchange(): pl.pallas_call(functools.partial(exchange_kernel, n, nc), out_shape=[jax....  31.7 us
    pallas_call x1, Pallas kernels, finish(): pl.pallas_call(functools.partial(finish_kernel, nc), grid=(members // mb,...  20.1 us
    unnamed x6, local copies, waits for them, and re-layouts  4 us

profile of v2, /device:TPU:5, one launch (start us, length us, event | category | flops | bytes accessed | tf_op | source)
XLA Modules:
  0.0 55.8 jit_solution(12936020365683500878)
XLA Ops:
  0.0 0.0 copy-start
  0.0 2.3 %copy-done = f32[24,16,24,128]{3,2,1,0:T(8,128)S(1)} copy-done((f32[24,16,24,128]{3,2,1,0:T(8,128)S(1)}, f32[24,16,24,128]{3,2,1,0:T(8,128)}, u32[]{:S(2)}) %copy-start) | copy-done | bytes 4718616
  2.3 0.0 copy-start.1
  2.3 1.0 %copy-done.1 = f32[24,24,128]{2,1,0:T(8,128)S(1)} copy-done((f32[24,24,128]{2,1,0:T(8,128)S(1)}, f32[24,24,128]{2,1,0:T(8,128)}, u32[]{:S(2)}) %copy-start.1) | copy-done | bytes 294936
  3.3 0.0 copy-start.2
  3.3 0.7 %copy-done.2 = f32[24,128]{1,0:T(8,128)S(1)} copy-done((f32[24,128]{1,0:T(8,128)S(1)}, f32[24,128]{1,0:T(8,128)}, u32[]{:S(2)}) %copy-start.2) | copy-done | bytes 12312
  4.0 31.7 %exchange.1 = (f32[24,16,8,128]{3,2,1,0:T(8,128)S(1)}, f32[24,8,128]{2,1,0:T(8,128)S(1)}, f32[8,128]{1,0:T(8,128)S(1)}, f32[4,16,24,128]{3,2,1,0:T(8,128)S(1)}, f32[4,16,8,128]{3,2,1,0:T(8,128)S(1)}) custom-call(f32[24,16,24,128]{3,2,1,0:T(8,128)S(1)} %copy-done, f32[24,24,128]{2,1,0:T(8,128)S(1)} %copy-done.1, f32[24,128]{1,0:T(8,128)S(1)} %copy-done.2), custom_call_target="tpu_custom_call" | custom-call | tf_op jit(solution)/shard_map/exchange/pallas_call | solution.py:290
  35.7 20.1 %finish.1 = f32[24,16,24,128]{3,2,1,0:T(8,128)} custom-call(f32[24,16,24,128]{3,2,1,0:T(8,128)S(1)} %copy-done, f32[24,16,8,128]{3,2,1,0:T(8,128)S(1)} %get-tuple-element.10.xh_ref, f32[24,24,128]{2,1,0:T(8,128)S(1)} %copy-done.1, f32[24,8,128]{2,1,0:T(8,128)S(1)} %get-tuple-element.11.wh_ref, f32[24,128]{1,0:T(8,128)S(1)} %copy-done.2, ...), custom_call_target="tpu_custom_call" | custom-call | tf_op jit(solution)/shard_map/finish/pallas_call | solution.py:405
Async XLA Ops:
  0.0 2.3 %copy-start = (f32[24,16,24,128]{3,2,1,0:T(8,128)S(1)}, f32[24,16,24,128]{3,2,1,0:T(8,128)}, u32[]{:S(2)}) copy-start(f32[24,16,24,128]{3,2,1,0:T(8,128)} %x_ref.1) | copy-start | bytes 14155780
  2.3 1.0 %copy-start.1 = (f32[24,24,128]{2,1,0:T(8,128)S(1)}, f32[24,24,128]{2,1,0:T(8,128)}, u32[]{:S(2)}) copy-start(f32[24,24,128]{2,1,0:T(8,128)} %w_ref.3) | copy-start | bytes 884740
  3.3 0.7 %copy-start.2 = (f32[24,128]{1,0:T(8,128)S(1)}, f32[24,128]{1,0:T(8,128)}, u32[]{:S(2)}) copy-start(f32[24,128]{1,0:T(8,128)} %k_ref.1) | copy-start | bytes 36868
